TPU v7x, 32 devices: a whole 2x2x4 slice. The times are simulated.
32 devices in a mesh: row: 8 (over z, y), col: 4 (over x, core).
Axes of the slice: x: 2, y: 2, z: 4, core: 2. Of those that a mesh axis runs over, the one named last changes fastest.
Arguments:
- grams: bfloat16 [4, 3584, 3584], P(None, 'row', 'col'), as said below
- weights: bfloat16 [4, 3584, 7168], P(None, 'row', 'col'), may hold values from -6 to 6
Outputs:
- merged: float32 [3584, 7168], P('row', 'col')
- residual: float32 [3584, 7168], P('row', 'col')
Inputs may be any that keep to these rules, and one draw needn't show every extreme that they name: `grams`: each of the 4 matrices is symmetric and positive definite.
All inputs are finite; a program needn't handle non-finite values.
Results may differ from a plain program's by a relative error of at most 0.012.
The roundings to bfloat16 on the way count: a program that leaves them out, or rounds other values in their place, can miss the bound.
Values may be sent and summed in bfloat16 or wider, within the bound.
A program may use at most 256 MiB of HBM per device.

v0:
```python
import jax
import jax.numpy as jnp
from jax import lax
from jax.sharding import PartitionSpec as P

ITERS = 2


def shards(grams, weights):
    slab_rows = grams.shape[1]
    col_count = weights.shape[2]
    first_row = lax.axis_index("row") * slab_rows
    high = lax.Precision.HIGHEST
    gram_slabs = lax.all_gather(grams, "col", axis=2, tiled=True)
    gram_total = jnp.sum(gram_slabs, axis=0, dtype=jnp.float32)
    square_block = lax.dynamic_slice_in_dim(gram_slabs, first_row, slab_rows, gram_slabs.ndim - 1)
    diag_total = jnp.einsum(
        "mr,mrc->rc",
        jnp.diagonal(square_block, axis1=-2, axis2=-1).astype(jnp.float32),
        weights.astype(jnp.float32),
    )
    product = lax.psum_scatter(
        jnp.einsum("mrk,mrc->kc", gram_slabs, weights, preferred_element_type=jnp.float32),
        "row",
        scatter_dimension=0,
        tiled=True,
    )
    right_side = 0.9 * product + 0.1 * diag_total
    total_diag = jnp.diagonal(lax.dynamic_slice_in_dim(gram_total, first_row, slab_rows, 1))
    merged = jnp.zeros((slab_rows, col_count), jnp.float32)
    residual = right_side
    direction = right_side

    def sum_squares(vector):
        return lax.psum(jnp.sum(vector * vector, axis=0), "row")

    norm_now = sum_squares(residual)
    for iteration in range(ITERS):
        rounded = direction.astype(jnp.bfloat16)
        shard_piece = lax.all_gather(rounded, "row", axis=0, tiled=True)
        add_columns = lax.slice_in_dim(gram_total, 0, shard_piece.shape[0], axis=1)
        mapped = jnp.zeros((slab_rows, col_count), jnp.float32) + jnp.dot(
            add_columns, shard_piece.astype(jnp.float32), precision=high
        )
        mapped = 0.9 * mapped + 0.1 * total_diag[:, None] * rounded.astype(jnp.float32)
        curvature = lax.psum(jnp.sum(direction * mapped, axis=0), "row")
        step_length = norm_now / curvature
        merged = merged + step_length * direction
        residual = residual - step_length * mapped
        if iteration + 1 < ITERS:
            norm_next = sum_squares(residual)
            direction = residual + norm_next / norm_now * direction
            norm_now = norm_next
    return (merged, residual)


def solution(mesh):
    placed = (P(None, "row", "col"), P(None, "row", "col"))
    return jax.shard_map(
        shards,
        mesh=mesh,
        in_specs=placed,
        out_specs=(P("row", "col"), P("row", "col")),
        check_vma=False,
    )
```

profile of v0, /device:TPU:0, one launch (start us, length us, event | category | flops | bytes accessed | tf_op | source)
XLA Modules:
  0.0 1040.9 jit_solution(6059432819298859422)
XLA Ops:
  7.2 0.7 all-gather.4.cloned.1.call-update
  7.9 87.8 %all-gather.4.cloned.1.call-done = bf16[4,448,3584]{2,1,0:T(8,128)(2,1)} async-done(((bf16[4,448,896]{2,1,0:T(8,128)(2,1)}), bf16[4,448,3584]{2,1,0:T(8,128)(2,1)}) %all-gather.4.cloned.1.call-update) | async-done | bytes 12845072 | tf_op jit(solution)/shard_map/all_gather | solution.py:14
  95.8 30.8 %convolution_bitcast_fusion = f32[3584,1792]{1,0:T(8,128)} fusion(bf16[4,448,3584]{2,1,0:T(8,128)(2,1)} %all-gather.4.cloned.1.call-done, bf16[4,448,1792]{2,1,0:T(8,128)(2,1)} %param.3), kind=kOutput, calls=%fused_computation.3 | convolution fusion | flops 23018340352 | bytes 44957696 | tf_op jit(solution)/shard_map/mrk,mrc->kc/dot_general | solution.py:23
  126.8 2.6 constant_dynamic-slice_fusion.1
  129.4 38.4 %copy.5 = bf16[4,448,448]{0,2,1:T(8,128)(2,1)} copy(bf16[4,448,448]{2,1,0:T(8,128)(2,1)S(1)} %constant_dynamic-slice_fusion.1) | data formatting | bytes 3211264 | tf_op jit(solution)/shard_map/dynamic_slice | solution.py:16
  167.8 8.7 gather_fusion
  176.5 19.1 %fusion = f32[448,1,1792]{2,1,0:T(1,128)} fusion(bf16[4,448,1792]{2,1,0:T(8,128)(2,1)} %param.3, bf16[4,448,1]{0,1,2:T(8,128)(2,1)S(1)} %bitcast.19), kind=kOutput, calls=%fused_computation.4 | convolution fusion | flops 6422528 | bytes 9637376 | tf_op jit(solution)/shard_map/mr,mrc->rc/dot_general | solution.py:17
  195.6 341.9 %reduce-scatter.2.cloned.1.call-done = f32[448,1792]{1,0:T(8,128)} async-done(((f32[3584,1792]{1,0:T(8,128)}), f32[448,1792]{1,0:T(8,128)}) %reduce-scatter.2.cloned.1.call-update) | async-done | bytes 3211280 | tf_op jit(solution)/shard_map/reduce_scatter | solution.py:22
  537.5 4.7 fusion.5
  542.2 0.3 all-gather.8.cloned.1.call-start
  542.5 10.3 convert_reduce_fusion
  552.8 2.6 copy-done
  555.4 1.2 constant_dynamic-slice_fusion
  556.7 7.6 gather_fusion.1
  564.3 156.5 %all-gather.6.cloned.1.call-done = bf16[3584,1792]{1,0:T(8,128)(2,1)} async-done(((bf16[448,1792]{1,0:T(8,128)(2,1)}), bf16[3584,1792]{1,0:T(8,128)(2,1)}) %all-gather.6.cloned.1.call-update) | async-done | bytes 12845072 | tf_op jit(solution)/shard_map/all_gather | solution.py:40
  720.8 25.4 %multiply_reduce_fusion.2 = (f32[1792]{0:T(1024)S(1)}, f32[1792]{0:T(1024)S(1)}, f32[448,1792]{1,0:T(8,128)}) fusion(f32[448,1792]{1,0:T(8,128)S(1)} %get-tuple-element.7, bf16[448,1792]{1,0:T(8,128)(2,1)} %get-tuple-element.6, f32[448]{0:T(512)S(1)} %broadcast_multiply_fusion, f32[448,3584]{1,0:T(8,128)} %copy-done, ...), kind=kOutput, calls=%fused_computation.15 | convolution fusion | flops 34533928960 | bytes 27311872 | tf_op jit(solution)/shard_map/dot_general | solution.py:42
  746.2 34.2 %all-reduce = (f32[1792]{0:T(1024)S(1)}, f32[1792]{0:T(1024)S(1)}) all-reduce(f32[1792]{0:T(1024)S(1)} %get-tuple-element.3, f32[1792]{0:T(1024)S(1)} %get-tuple-element.2), channel_id=1, replica_groups=mesh['row'=8,'col'=4] {'row'}, use_global_device_ids=true, to_apply=%region_2.3 | all-reduce | flops 3584 | bytes 28672 | tf_op jit(solution)/shard_map/psum | solution.py:35
  780.4 2.4 multiply_reduce_fusion.1
  782.7 17.6 %psum.30 = f32[1792]{0:T(1024)S(1)} all-reduce(f32[1792]{0:T(1024)S(1)} %multiply_reduce_fusion.1), channel_id=1, replica_groups=mesh['row'=8,'col'=4] {'row'}, use_global_device_ids=true, to_apply=%region_7.8 | all-reduce | flops 1792 | bytes 14336 | tf_op jit(solution)/shard_map/psum | solution.py:35
  800.4 3.5 fusion.4
  803.9 178.1 %all-gather.8.cloned.1.call-done = bf16[3584,1792]{1,0:T(8,128)(2,1)} async-done(((bf16[448,1792]{1,0:T(8,128)(2,1)}), bf16[3584,1792]{1,0:T(8,128)(2,1)}) %all-gather.8.cloned.1.call-update) | async-done | bytes 12845072 | tf_op jit(solution)/shard_map/all_gather | solution.py:40
  982.1 26.5 %multiply_reduce_fusion = (f32[1792]{0:T(1024)S(1)}, f32[448,1792]{1,0:T(8,128)}) fusion(f32[448,1792]{1,0:T(8,128)S(1)} %get-tuple-element.7, f32[1792]{0:T(1024)S(1)} %div.10, f32[448,1792]{1,0:T(8,128)} %get-tuple-element.10, f32[1792]{0:T(1024)S(1)} %div.9, bf16[448,1792]{1,0:T(8,128)(2,1)} %fusion.4, f32[448]{0:T(512)S(1)} %broadcast_multiply_fusion, ...), kind=kOutput, calls=%fused_computation.10 | convolution fusion | flops 34535538688 | bytes 30530304 | tf_op jit(solution)/shard_map/dot_general | solution.py:42
  1008.6 18.7 %psum.31 = f32[1792]{0:T(1024)S(1)} all-reduce(f32[1792]{0:T(1024)S(1)} %get-tuple-element.11), channel_id=1, replica_groups=mesh['row'=8,'col'=4] {'row'}, use_global_device_ids=true, to_apply=%region_9.10 | all-reduce | flops 1792 | bytes 14336 | tf_op jit(solution)/shard_map/psum | solution.py:46
  1027.3 6.6 multiply_subtract_fusion
  (12 shorter events, 0.4 us)
Async XLA Ops:
  7.2 88.6 %all-gather.4.cloned.1.call-start = ((), (), s32[]{:S(2)}) async-start(), calls=%async_computation.1 | async-start | bytes 16056320 | tf_op jit(solution)/shard_map/all_gather | solution.py:14
  7.9 529.7 %reduce-scatter.2.cloned.1.call-start = ((), (), s32[]{:S(2)}) async-start(), calls=%async_computation.2 | async-start | bytes 28901376 | tf_op jit(solution)/shard_map/reduce_scatter | solution.py:22
  126.6 594.2 %all-gather.6.cloned.1.call-start = ((), (), s32[]{:S(2)}) async-start(), calls=%async_computation.3 | async-start | bytes 14450688 | tf_op jit(solution)/shard_map/all_gather | solution.py:40
  542.2 439.9 %all-gather.8.cloned.1.call-start = ((), (), s32[]{:S(2)}) async-start(), calls=%async_computation.4 | async-start | bytes 14450688 | tf_op jit(solution)/shard_map/all_gather | solution.py:40
  552.8 2.6 copy-start
Sparse Core Ops, SparseCore 0:
  9.5 86.1 all-gather.3
  126.7 410.7 reduce-scatter.1
  542.4 178.4 all-gather.5
  804.1 177.9 all-gather.7
where the time goes:
time: 1050 us; the launch traced here: 1040 us
  waiting for transfers between devices  765 us (73%)
  matrix products  102 us (10%)
  blocking collectives  70.6 us (7%)
  local copies, waits for them, and re-layouts  61.1 us (6%)
  other arithmetic  27.5 us (3%)
  between operations  14.3 us (1%)
    reduce_scatter x1, waiting for transfers between devices, shards(): lax.psum_scatter(jnp.einsum('mrk,mrc->kc', gram_slabs, weights, preferred...  342 us
    all_gather x2, waiting for transfers between devices, shards(): shard_piece = lax.all_gather(rounded, 'row', axis=0, tiled=True)  335 us
    all_gather x1, waiting for transfers between devices, shards(): gram_slabs = lax.all_gather(grams, 'col', axis=2, tiled=True)  87.8 us
    dot_general x2, matrix products, shards(): jnp.dot(add_columns, shard_piece.astype(jnp.float32), precision=high)  51.8 us
    psum x2, blocking collectives, sum_squares(): return lax.psum(jnp.sum(vector * vector, axis=0), 'row')  51.8 us
    dynamic_slice x2, local copies, waits for them, and re-layouts, shards(): lax.dynamic_slice_in_dim(gram_slabs, first_row, slab_rows, gram_slabs.ndi...  40.9 us
    dot_general x1, matrix products, shards(): jnp.einsum('mrk,mrc->kc', gram_slabs, weights, preferred_element_type=jnp...  30.8 us
  transfers between devices with their start and end apart: 4, of which 4 were waited for; matrix products, arithmetic and copies ran while one was open for 8% of the time, Pallas kernels for 0%

commit v1 on v0

v1 whole, which is shorter than its diff:
```python
import functools

import jax
import jax.numpy as jnp
from jax import lax
from jax.experimental import pallas as pl
from jax.experimental.pallas import tpu as pltpu
from jax.sharding import PartitionSpec as P

ITERS = 2
STREAMS = 2
MESH = pl.DeviceIdType.MESH


def ring_position(index, n):
    odd = index % 2
    return (1 - odd) * (index // 2) + odd * (n - 1 - index // 2)


def ring_index(position, n):
    back = position // (n // 2)
    return (1 - back) * 2 * position + back * (2 * (n - 1 - position) + 1)


def ring_product_kernel(n, x_ref, high_ref, low_ref, out_ref, ahead, behind, send_a, recv_a, send_b, recv_b):
    me = lax.axis_index("row")
    place = ring_position(me, n)
    right = ring_index((place + 1) % n, n)
    left = ring_index((place + n - 1) % n, n)
    half, columns = ahead.shape[2], x_ref.shape[1]

    barrier = pltpu.get_barrier_semaphore()
    for other in (left, right):
        pl.semaphore_signal(barrier, inc=1, device_id={"row": other}, device_id_type=MESH)
    pl.semaphore_wait(barrier, 2)

    def send(source, held, slot, sends, recvs, target):
        return pltpu.make_async_remote_copy(
            src_ref=source,
            dst_ref=held.at[slot],
            send_sem=sends.at[slot],
            recv_sem=recvs.at[slot],
            device_id={"row": target},
            device_id_type=MESH,
        )

    def add(where, owner, block):
        out_ref[:, where] += jnp.dot(high_ref[owner], block, preferred_element_type=jnp.float32) + jnp.dot(
            low_ref[owner], block, preferred_element_type=jnp.float32
        )

    front, rest = slice(0, half), slice(half, columns)
    send(x_ref.at[:, pl.ds(0, half)], ahead, 0, send_a, recv_a, right).start()
    send(x_ref.at[:, pl.ds(half, columns - half)], behind, 0, send_b, recv_b, left).start()
    out_ref[...] = jnp.zeros_like(out_ref)
    add(front, me, x_ref[:, front])
    add(rest, me, x_ref[:, rest])

    def step(s, carry):
        send(ahead.at[s], ahead, s, send_a, recv_a, right).wait()
        send(behind.at[s], behind, s, send_b, recv_b, left).wait()

        @pl.when(s < n - 2)
        def _():
            send(ahead.at[s], ahead, s + 1, send_a, recv_a, right).start()
            send(behind.at[s], behind, s + 1, send_b, recv_b, left).start()

        add(front, ring_index((place + n - 1 - s) % n, n), ahead[s])
        add(rest, ring_index((place + 1 + s) % n, n), behind[s])
        return carry

    lax.fori_loop(0, n - 1, step, 0)


def ring_product(n, rounded, high, low):
    rows, columns = rounded.shape
    half = pl.cdiv(columns, 256) * 128
    held = [pltpu.VMEM((n - 1, rows, size), jnp.bfloat16) for size in (half, columns - half)]
    return pl.pallas_call(
        functools.partial(ring_product_kernel, n),
        out_shape=jax.ShapeDtypeStruct((rows, columns), jnp.float32),
        in_specs=[pl.BlockSpec(memory_space=pltpu.VMEM)] * 3,
        out_specs=pl.BlockSpec(memory_space=pltpu.VMEM),
        scratch_shapes=held + [pltpu.SemaphoreType.DMA((n - 1,))] * 4,
        compiler_params=pltpu.CompilerParams(collective_id=1, has_side_effects=True, vmem_limit_bytes=48 * 2**20),
    )(rounded, high, low)


def row_sum_kernel(n, x_ref, out_ref, held, sends, recvs):
    me = lax.axis_index("row")
    barrier = pltpu.get_barrier_semaphore()
    for k in range(1, n):
        pl.semaphore_signal(barrier, inc=1, device_id={"row": (me + k) % n}, device_id_type=MESH)
    pl.semaphore_wait(barrier, n - 1)
    copies = []
    for k in range(1, n):
        copy = pltpu.make_async_remote_copy(
            src_ref=x_ref,
            dst_ref=held.at[k - 1],
            send_sem=sends.at[k - 1],
            recv_sem=recvs.at[k - 1],
            device_id={"row": (me + k) % n},
            device_id_type=MESH,
        )
        copy.start()
        copies.append(copy)
    for copy in copies:
        copy.wait()
    total = x_ref[...]
    for k in range(n - 1):
        total = total + held[k]
    out_ref[...] = total


def row_sum(n, values):
    flat = values.reshape(-1, 128)
    return pl.pallas_call(
        functools.partial(row_sum_kernel, n),
        out_shape=jax.ShapeDtypeStruct(flat.shape, jnp.float32),
        in_specs=[pl.BlockSpec(memory_space=pltpu.VMEM)],
        out_specs=pl.BlockSpec(memory_space=pltpu.VMEM),
        scratch_shapes=[pltpu.VMEM((n - 1,) + flat.shape, jnp.float32)] + [pltpu.SemaphoreType.DMA((n - 1,))] * 2,
        compiler_params=pltpu.CompilerParams(collective_id=2, has_side_effects=True),
    )(flat).reshape(values.shape)


def shards(row_count, grams, weights):
    models, slab_rows, slab_cols = grams.shape
    col_count = weights.shape[2]
    row_index = lax.axis_index("row")
    first_row = row_index * slab_rows
    width = col_count // STREAMS

    gathered = lax.all_gather(grams, "col", axis=0)
    parts = gathered.shape[0]

    def own_columns(array):
        per_slab = slab_cols // slab_rows
        slab = lax.dynamic_index_in_dim(array, row_index // per_slab, 0, keepdims=False)
        offset = (row_index % per_slab) * slab_rows
        return lax.dynamic_slice_in_dim(slab, offset, slab_rows, slab.ndim - 1)

    block = own_columns(gathered)
    on_diag = jnp.arange(slab_rows)[:, None] == jnp.arange(slab_rows)[None, :]
    diags = jnp.sum(jnp.where(on_diag, block.astype(jnp.float32), 0.0), axis=2)
    total_diag = jnp.sum(diags, axis=0)
    total = jnp.sum(gathered.astype(jnp.float32), axis=1)
    total = total.reshape(parts, slab_rows, -1, slab_rows).swapaxes(1, 2).reshape(row_count, slab_rows, slab_rows)
    high = total.astype(jnp.bfloat16)
    low = (total - high.astype(jnp.float32)).astype(jnp.bfloat16)
    first_part = (((0,), (0,)), ((), ()))
    depth = models * slab_rows
    flat = gathered.reshape(parts, depth, slab_cols)
    flat_block = block.reshape(depth, slab_rows)
    in_block = (jnp.arange(parts * slab_cols) // slab_rows) == row_index

    def right_side(weight):
        flat_weight = weight.reshape(depth, width)
        pieces = []
        for d in range(parts):
            piece = lax.dot_general(flat[d], flat_weight, first_part, preferred_element_type=jnp.float32)
            keep = in_block[d * slab_cols : (d + 1) * slab_cols]
            pieces.append(jnp.where(keep[:, None], 0.0, piece).astype(jnp.bfloat16))
        others = lax.psum_scatter(jnp.concatenate(pieces, axis=0), "row", scatter_dimension=0, tiled=True)
        own = lax.dot_general(flat_block, flat_weight, first_part, preferred_element_type=jnp.float32)
        diag_term = jnp.sum(diags[:, :, None] * weight.astype(jnp.float32), axis=0)
        return 0.9 * (own + others.astype(jnp.float32)) + 0.1 * diag_term

    def column_sum(values):
        return row_sum(row_count, jnp.sum(values, axis=0))

    starts = [right_side(lax.slice_in_dim(weights, s * width, (s + 1) * width, axis=2)) for s in range(STREAMS)]
    residual = jnp.concatenate(starts, axis=1)
    direction = residual
    merged = jnp.zeros_like(residual)
    norm_now = column_sum(residual * residual)
    for iteration in range(ITERS):
        rounded = direction.astype(jnp.bfloat16)
        product = ring_product(row_count, rounded, high, low)
        mapped = 0.9 * product + 0.1 * total_diag[:, None] * rounded.astype(jnp.float32)
        curvature = column_sum(direction * mapped)
        step_length = norm_now / curvature
        merged = merged + step_length * direction
        residual = residual - step_length * mapped
        if iteration + 1 < ITERS:
            norm_next = column_sum(residual * residual)
            direction = residual + norm_next / norm_now * direction
            norm_now = norm_next
    return merged, residual


def solution(mesh):
    placed = (P(None, "row", "col"), P(None, "row", "col"))
    return jax.shard_map(
        functools.partial(shards, mesh.shape["row"]),
        mesh=mesh,
        in_specs=placed,
        out_specs=(P("row", "col"), P("row", "col")),
        check_vma=False,
    )
```

time: 1050 us -> 699 us (0.67)
  waiting for transfers between devices: 765 us -> 266 us
  Pallas kernels: 0 us -> 294 us
  blocking collectives: 70.6 us -> 0 us
  matrix products: 102 us -> 48.7 us
  local copies, waits for them, and re-layouts: 61.1 us -> 14.2 us
  other arithmetic: 27.5 us -> 54.8 us
    all_gather x3 -> x1, waiting for transfers between devices: 422 us -> 82.8 us  [shards(): gathered = lax.all_gather(grams, 'col', axis=0)]
    pallas_call x0 -> x6, Pallas kernels: none -> 294 us  [the longest x2 263 us: ring_product(): pl.pallas_call(functools.partial(ring_product_kernel, n), out_shape=jax.S...]
    reduce_scatter x1 -> x2, waiting for transfers between devices: 342 us -> 183 us  [right_side(): lax.psum_scatter(jnp.concatenate(pieces, axis=0), 'row', scatter_dimensio...]
    psum x3 -> x0, blocking collectives: 70.6 us -> none  [the longest x2 51.8 us: sum_squares(): return lax.psum(jnp.sum(vector * vector, axis=0), 'row')]
    dot_general x4 -> x10, matrix products: 102 us -> 48.7 us  [the longest x8 39.7 us: right_side(): lax.dot_general(flat[d], flat_weight, first_part, preferred_element_type=...]
    dynamic_slice x3 -> x0, local copies, waits for them, and re-layouts: 42.2 us -> none  [the longest x2 40.9 us: shards(): lax.dynamic_slice_in_dim(gram_slabs, first_row, slab_rows, gram_slabs.ndi...]
    gather x2 -> x0, local copies, waits for them, and re-layouts: 16.4 us -> none  [the longest x1 8.72 us: shards(): jnp.diagonal(square_block, axis1=-2, axis2=-1).astype(jnp.float32)]
    concatenate x1 -> x3, other arithmetic: 0.01 us -> 15.2 us  [the longest x2 12.2 us: right_side(): jnp.concatenate(pieces, axis=0)]
  transfers between devices with their start and end apart: 4 -> 3, of which waited for: 4 -> 3; matrix products, arithmetic and copies ran while one was open for 8% -> 9% of each run, Pallas kernels for 0% -> 0%
where the time goes in v1:
time: 699 us; the launch traced here: 693 us
  Pallas kernels  294 us (42%)
  waiting for transfers between devices  266 us (38%)
  other arithmetic  54.8 us (8%)
  matrix products  48.7 us (7%)
  between operations  14.6 us (2%)
  local copies, waits for them, and re-layouts  14.2 us (2%)
    pallas_call x2, Pallas kernels, ring_product(): pl.pallas_call(functools.partial(ring_product_kernel, n), out_shape=jax.S...  263 us
    reduce_scatter x2, waiting for transfers between devices, right_side(): lax.psum_scatter(jnp.concatenate(pieces, axis=0), 'row', scatter_dimensio...  183 us
    all_gather x1, waiting for transfers between devices, shards(): gathered = lax.all_gather(grams, 'col', axis=0)  82.8 us
    dot_general x8, matrix products, right_side(): lax.dot_general(flat[d], flat_weight, first_part, preferred_element_type=...  39.7 us
    pallas_call x4, Pallas kernels, row_sum(): pl.pallas_call(functools.partial(row_sum_kernel, n), out_shape=jax.ShapeD...  31.1 us
  transfers between devices with their start and end apart: 3, of which 3 were waited for; matrix products, arithmetic and copies ran while one was open for 9% of the time, Pallas kernels for 0%

profile of v1, /device:TPU:0, one launch (start us, length us, event | category | flops | bytes accessed | tf_op | source)
XLA Modules:
  0.0 692.5 jit_solution(2484154185009685751)
XLA Ops:
  8.0 5.1 fusion.10
  13.1 82.8 %all-gather.3.cloned.1.call-done = bf16[16,448,896]{2,1,0:T(8,128)(2,1)} async-done(((bf16[4,448,896]{2,1,0:T(8,128)(2,1)}), bf16[16,448,896]{2,1,0:T(8,128)(2,1)}) %all-gather.3.cloned.1.call-update) | async-done | bytes 12845072 | tf_op jit(solution)/shard_map/all_gather | solution.py:134
  95.9 5.7 fusion.8
  101.7 5.2 select_convert_fusion
  106.8 4.6 select_convert_fusion.1
  111.4 4.6 select_convert_fusion.2
  116.1 4.6 select_convert_fusion.3
  120.7 6.0 pad_maximum_fusion.2
  127.0 6.7 select_convert_fusion.4
  133.7 4.6 select_convert_fusion.5
  138.3 4.7 select_convert_fusion.6
  143.0 4.6 select_convert_fusion.7
  147.6 6.1 pad_maximum_fusion.1
  157.6 10.4 %convert_reduce_fusion = f32[4,448,896]{2,1,0:T(8,128)S(1)} fusion(bf16[16,448,896]{2,1,0:T(8,128)(2,1)} %all-gather.3.cloned.1.call-done), kind=kLoop, calls=%fused_computation | loop fusion | flops 11239424 | bytes 19267584 | tf_op jit(solution)/shard_map/reduce_sum | solution.py:147
  182.2 64.6 %reduce-scatter.5.cloned.1.call-done = bf16[448,896]{1,0:T(8,128)(2,1)} async-done(((bf16[3584,896]{1,0:T(8,128)(2,1)}), bf16[448,896]{1,0:T(8,128)(2,1)}) %reduce-scatter.5.cloned.1.call-update) | async-done | bytes 802832 | tf_op jit(solution)/shard_map/reduce_scatter | solution.py:164
  251.4 118.2 %reduce-scatter.3.cloned.1.call-done = bf16[448,896]{1,0:T(8,128)(2,1)} async-done(((bf16[3584,896]{1,0:T(8,128)(2,1)}), bf16[448,896]{1,0:T(8,128)(2,1)}) %reduce-scatter.3.cloned.1.call-update) | async-done | bytes 802832 | tf_op jit(solution)/shard_map/reduce_scatter | solution.py:164
  369.6 4.5 multiply_add_fusion.5
  374.3 130.9 %shard_map.42 = f32[448,1792]{1,0:T(8,128)S(1)} custom-call(bf16[448,1792]{1,0:T(8,128)(2,1)S(1)} %fusion.7.x_ref, bf16[8,448,448]{2,1,0:T(8,128)(2,1)} %get-tuple-element.9.high_ref, bf16[8,448,448]{2,1,0:T(8,128)(2,1)} %get-tuple-element.8.low_ref), custom_call_target="tpu_custom_call" | custom-call | tf_op jit(solution)/shard_map/pallas_call | solution.py:79
  506.7 7.8 %shard_map.43 = f32[14,128]{1,0:T(8,128)} custom-call(f32[14,128]{1,0:T(8,128)} %bitcast.69), custom_call_target="tpu_custom_call" | custom-call | tf_op jit(solution)/shard_map/pallas_call | solution.py:117
  514.5 7.8 %shard_map.41 = f32[14,128]{1,0:T(8,128)} custom-call(f32[14,128]{1,0:T(8,128)} %bitcast.68), custom_call_target="tpu_custom_call" | custom-call | tf_op jit(solution)/shard_map/pallas_call | solution.py:117
  526.4 7.8 %shard_map.44 = f32[14,128]{1,0:T(8,128)} custom-call(f32[14,128]{1,0:T(8,128)} %bitcast.70), custom_call_target="tpu_custom_call" | custom-call | tf_op jit(solution)/shard_map/pallas_call | solution.py:117
  537.7 131.6 %shard_map.45 = f32[448,1792]{1,0:T(8,128)S(1)} custom-call(bf16[448,1792]{1,0:T(8,128)(2,1)S(1)} %fusion.2.x_ref, bf16[8,448,448]{2,1,0:T(8,128)(2,1)} %get-tuple-element.9.high_ref, bf16[8,448,448]{2,1,0:T(8,128)(2,1)} %get-tuple-element.8.low_ref), custom_call_target="tpu_custom_call" | custom-call | tf_op jit(solution)/shard_map/pallas_call | solution.py:79
  671.6 7.8 %shard_map.46 = f32[14,128]{1,0:T(8,128)} custom-call(f32[14,128]{1,0:T(8,128)} %bitcast.71), custom_call_target="tpu_custom_call" | custom-call | tf_op jit(solution)/shard_map/pallas_call | solution.py:117
  680.1 5.5 multiply_subtract_fusion
  (63 shorter events, 35.6 us)
Async XLA Ops:
  7.2 88.7 %all-gather.3.cloned.1.call-start = ((), (), s32[]{:S(2)}) async-start(), calls=%async_computation.4 | async-start | bytes 16056320 | tf_op jit(solution)/shard_map/all_gather | solution.py:134
  7.9 238.9 %reduce-scatter.5.cloned.1.call-start = ((), (), s32[]{:S(2)}) async-start(), calls=%async_computation.3 | async-start | bytes 7225344 | tf_op jit(solution)/shard_map/reduce_scatter | solution.py:164
  13.1 129.9 %copy-start.6 = (bf16[4,448,896]{2,1,0:T(8,128)(2,1)}, bf16[4,448,896]{2,1,0:T(8,128)(2,1)S(1)}, u32[]{:S(2)}) copy-start(bf16[4,448,896]{2,1,0:T(8,128)(2,1)S(1)} %get-tuple-element.19) | copy-start | bytes 9633796
  95.9 5.8 copy-start.7
  101.6 5.2 copy-start.12
  101.6 9.8 %copy-start.14 = (bf16[4,448,896]{2,1,0:T(8,128)(2,1)}, bf16[4,448,896]{2,1,0:T(8,128)(2,1)S(1)}, u32[]{:S(2)}) copy-start(bf16[4,448,896]{2,1,0:T(8,128)(2,1)S(1)} %get-tuple-element.12) | copy-start | bytes 9633796
  101.6 9.8 %copy-start.10 = (bf16[4,448,896]{2,1,0:T(8,128)(2,1)}, bf16[4,448,896]{2,1,0:T(8,128)(2,1)S(1)}, u32[]{:S(2)}) copy-start(bf16[4,448,896]{2,1,0:T(8,128)(2,1)S(1)} %get-tuple-element.14) | copy-start | bytes 9633796
  101.6 14.4 %copy-start.8 = (bf16[4,448,896]{2,1,0:T(8,128)(2,1)}, bf16[4,448,896]{2,1,0:T(8,128)(2,1)S(1)}, u32[]{:S(2)}) copy-start(bf16[4,448,896]{2,1,0:T(8,128)(2,1)S(1)} %get-tuple-element.11) | copy-start | bytes 9633796
  126.7 242.9 %reduce-scatter.3.cloned.1.call-start = ((), (), s32[]{:S(2)}) async-start(), calls=%async_computation.2 | async-start | bytes 7225344 | tf_op jit(solution)/shard_map/reduce_scatter | solution.py:164
  127.0 6.7 copy-start.13
  133.7 4.6 copy-start.11
  138.3 4.7 copy-start.9
  168.0 6.3 slice-start
  171.3 3.1 slice-start.1
  251.3 122.8 %copy-start.1 = (f32[448,896]{1,0:T(8,128)}, f32[448,896]{1,0:T(8,128)S(1)}, u32[]{:S(2)}) copy-start(f32[448,896]{1,0:T(8,128)S(1)} %multiply_add_fusion.4) | copy-start | bytes 4816900
  374.1 131.1 %copy-start.4 = (f32[448,896]{1,0:T(8,128)}, f32[448,896]{1,0:T(8,128)S(1)}, u32[]{:S(2)}) copy-start(f32[448,896]{1,0:T(8,128)S(1)} %multiply_add_fusion.5) | copy-start | bytes 4816900
  374.3 131.0 %copy-start.2 = (f32[448,896]{1,0:T(8,128)S(1)}, f32[448,896]{1,0:T(8,128)}, u32[]{:S(2)}) copy-start(f32[448,896]{1,0:T(8,128)} %copy-done.1) | copy-start | bytes 4816900
  523.0 11.2 %copy-start.16 = (f32[14,128]{1,0:T(8,128)S(1)}, f32[14,128]{1,0:T(8,128)}, u32[]{:S(2)}) copy-start(f32[14,128]{1,0:T(8,128)} %shard_map.41) | copy-start | bytes 21508
  537.7 131.7 %copy-start.3 = (f32[448,896]{1,0:T(8,128)S(1)}, f32[448,896]{1,0:T(8,128)}, u32[]{:S(2)}) copy-start(f32[448,896]{1,0:T(8,128)} %copy-done.1) | copy-start | bytes 4816900
  537.7 131.7 %copy-start.5 = (f32[448,896]{1,0:T(8,128)S(1)}, f32[448,896]{1,0:T(8,128)}, u32[]{:S(2)}) copy-start(f32[448,896]{1,0:T(8,128)} %copy-done.4) | copy-start | bytes 4816900
  669.4 2.2 copy-start
  669.4 10.0 %copy-start.15 = (f32[14,128]{1,0:T(8,128)S(1)}, f32[14,128]{1,0:T(8,128)}, u32[]{:S(2)}) copy-start(f32[14,128]{1,0:T(8,128)} %shard_map.44) | copy-start | bytes 21508
Sparse Core Ops, SparseCore 0:
  9.5 86.2 all-gather.2
  126.9 119.9 reduce-scatter.4
  250.4 119.1 reduce-scatter.2
